TPU v7x, 32 devices: a whole 2x2x4 slice. The times are simulated.
32 devices in a mesh: dp: 8 (over z, x), fsdp: 4 (over y, core).
Axes of the slice: x: 2, y: 2, z: 4, core: 2. Of those that a mesh axis runs over, the one named last changes fastest.
Arguments:
- queries: bfloat16 [8192, 768], P(('dp', 'fsdp')), may hold values from -6 to 6
- keys_values: bfloat16 [8192, 256], P(('dp', 'fsdp')), may hold values from -6 to 6
- seg_ids: int32 [8192], P(('dp', 'fsdp')), may hold values from 0 to 8191, as said below
- in_resp: int32 [8192], P(('dp', 'fsdp')), may hold values from 0 to 1, as said below
- advantage: int32 [8192], P(('dp', 'fsdp')), may hold values from -24 to 24
- out_weight: bfloat16 [768, 1536], P(None, 'fsdp'), may hold values from -0.21875 to 0.21875
- upstream: bfloat16 [8192, 1536], P(('dp', 'fsdp')), may hold values from -6 to 6
Outputs:
- branch_out: bfloat16 [8192, 1536], P(('dp', 'fsdp'))
- grad_queries: bfloat16 [8192, 768], P(('dp', 'fsdp'))
- grad_keys_values: bfloat16 [8192, 256], P(('dp', 'fsdp'))
- grad_weight: float32 [768, 1536], P('dp', 'fsdp')
Inputs may be any that keep to these rules, and one draw needn't show every extreme that they name: `seg_ids`: never falling; a token's id is the position of the first token of its sequence; a new sequence begins at the first of every 256 tokens, so no sequence spans two devices. `in_resp`: the last of every 256 tokens is 1.
All inputs are finite; a program needn't handle non-finite values.
Results may differ from a plain program's by a relative error of at most 0.012.
Values may be sent and summed in bfloat16 or wider, within the bound.
A program may use at most 64 MiB of HBM per device.

v0:
```python
import jax
import jax.numpy as jnp
from jax import lax
from jax.sharding import PartitionSpec as P

neg_fill = -1e30


def attend_forward(q_rows, kv_rows, seg_rows):
    count = q_rows.shape[0]
    head = kv_rows.shape[1] // 2
    heads = q_rows.shape[1] // head
    keys = kv_rows[:, :head]
    values = kv_rows[:, head:]
    place = jnp.arange(count, dtype=jnp.int32)
    allowed = (seg_rows[:, None] == seg_rows[None, :]) & (place[None, :] <= place[:, None])
    scale = head ** (-0.5)
    outputs = []
    probs = []
    for index in range(heads):
        q_head = q_rows[:, index * head : (index + 1) * head]
        scores = (
            lax.dot_general(
                q_head, keys, (((1,), (1,)), ((), ())), preferred_element_type=jnp.float32
            )
            * scale
        )
        scores = jnp.where(allowed, scores, neg_fill)
        top = jnp.max(scores, axis=1, keepdims=True)
        expo = jnp.exp(scores - top)
        prob = expo / jnp.sum(expo, axis=1, keepdims=True)
        outputs.append(
            jnp.dot(prob.astype(jnp.bfloat16), values, preferred_element_type=jnp.float32)
        )
        probs.append(prob)
    return (jnp.concatenate(outputs, axis=1).astype(jnp.bfloat16), probs)


def attend_backward(q_rows, kv_rows, attn_rows, d_attn, probs):
    count = q_rows.shape[0]
    head = kv_rows.shape[1] // 2
    heads = q_rows.shape[1] // head
    keys = kv_rows[:, :head]
    values = kv_rows[:, head:]
    scale = head ** (-0.5)
    grad_parts = []
    grad_keys = jnp.zeros((count, head), jnp.float32)
    grad_values = jnp.zeros((count, head), jnp.float32)
    for index in range(heads):
        cols = slice(index * head, (index + 1) * head)
        q_head = q_rows[:, cols]
        d_head = d_attn[:, cols]
        delta = jnp.sum(
            d_head.astype(jnp.float32) * attn_rows[:, cols].astype(jnp.float32),
            axis=1,
            keepdims=True,
        )
        d_prob = lax.dot_general(
            d_head, values, (((1,), (1,)), ((), ())), preferred_element_type=jnp.float32
        )
        d_score = (probs[index] * (d_prob - delta)).astype(jnp.bfloat16)
        grad_parts.append(jnp.dot(d_score, keys, preferred_element_type=jnp.float32) * scale)
        grad_keys = (
            grad_keys
            + lax.dot_general(
                d_score, q_head, (((0,), (0,)), ((), ())), preferred_element_type=jnp.float32
            )
            * scale
        )
        grad_values = grad_values + lax.dot_general(
            probs[index].astype(jnp.bfloat16),
            d_head,
            (((0,), (0,)), ((), ())),
            preferred_element_type=jnp.float32,
        )
    grad_q = jnp.concatenate(grad_parts, axis=1).astype(jnp.bfloat16)
    grad_kv = jnp.concatenate([grad_keys, grad_values], axis=1).astype(jnp.bfloat16)
    return (grad_q, grad_kv)


def on_device(queries, keys_values, seg_ids, in_resp, advantage, out_weight, upstream):
    attn_rows, probs = attend_forward(queries, keys_values, seg_ids)
    whole_weight = lax.all_gather(out_weight, "fsdp", axis=1, tiled=True)
    branch = jnp.dot(attn_rows, whole_weight, preferred_element_type=jnp.float32)
    branch_out = branch.astype(jnp.bfloat16)
    resp_total = lax.psum(jnp.sum(in_resp), ("dp", "fsdp"))
    all_tokens = queries.shape[0] * lax.axis_size("dp") * lax.axis_size("fsdp")
    factor = -(jnp.float32(all_tokens) / resp_total.astype(jnp.float32))
    coef = factor * in_resp.astype(jnp.float32) * (advantage.astype(jnp.float32) * 0.125)
    d_out = (coef[:, None] * upstream.astype(jnp.float32)).astype(jnp.bfloat16)
    d_attn = lax.dot_general(
        d_out, whole_weight, (((1,), (1,)), ((), ())), preferred_element_type=jnp.float32
    )
    d_attn = d_attn.astype(jnp.bfloat16)
    partial_value = lax.dot_general(
        attn_rows, d_out, (((0,), (0,)), ((), ())), preferred_element_type=jnp.float32
    )
    column_sums = lax.psum_scatter(
        partial_value.astype(jnp.bfloat16), "fsdp", scatter_dimension=1, tiled=True
    ).astype(jnp.float32)
    grad_weight = lax.psum_scatter(column_sums, "dp", scatter_dimension=0, tiled=True)
    grad_q, grad_kv = attend_backward(queries, keys_values, attn_rows, d_attn, probs)
    return (branch_out, grad_q, grad_kv, grad_weight)


def solution(mesh):
    in_specs = (
        P(("dp", "fsdp"), None),
        P(("dp", "fsdp"), None),
        P(("dp", "fsdp")),
        P(("dp", "fsdp")),
        P(("dp", "fsdp")),
        P(None, "fsdp"),
        P(("dp", "fsdp"), None),
    )
    out_specs = (
        P(("dp", "fsdp"), None),
        P(("dp", "fsdp"), None),
        P(("dp", "fsdp"), None),
        P("dp", "fsdp"),
    )
    return jax.shard_map(
        on_device, mesh=mesh, in_specs=in_specs, out_specs=out_specs, check_vma=False
    )
```

profile of v0, /device:TPU:0, one launch (start us, length us, event | category | flops | bytes accessed | tf_op | source)
XLA Modules:
  0.0 174.3 jit_solution(16585435467374152783)
XLA Ops:
  7.2 0.7 all-gather.2.cloned.1.call-update
  8.0 1.1 fusion.113
  9.1 1.2 fusion.114
  10.3 1.2 fusion.115
  11.5 1.4 reduce_sum.123
  13.0 42.7 %psum.7 = s32[]{:T(128)} all-reduce(s32[]{:T(128)} %reduce_sum.123), channel_id=1, replica_groups=mesh['dp'=8,'fsdp'=4] {'dp','fsdp'}, use_global_device_ids=true, to_apply=%region_13.14 | all-reduce | flops 1 | bytes 8 | tf_op jit(solution)/shard_map/psum | solution.py:86
  57.5 0.9 constant_dynamic-update-slice_fusion.5
  58.4 0.8 constant_dynamic-update-slice_fusion.4
  59.2 0.9 constant_dynamic-update-slice_fusion.3
  60.1 0.8 constant_dynamic-update-slice_fusion.2
  61.0 0.9 constant_dynamic-update-slice_fusion.1
  61.8 0.8 constant_dynamic-update-slice_fusion
  62.7 0.9 convolution_convert_fusion
  63.6 2.5 %copy.36 = bf16[768,1536]{0,1:T(8,128)(2,1)} copy(bf16[768,1536]{1,0:T(8,128)(2,1)S(1)} %convolution_convert_fusion) | data formatting | bytes 4718592
  66.2 0.9 copy-done.2
  67.2 2.5 %convolution_convert_fusion.2 = bf16[256,768]{0,1:T(8,128)(2,1)S(1)} fusion(bf16[768,1536]{1,0:T(8,128)(2,1)} %all-gather.2.cloned.1.call-done, bf16[256,1536]{1,0:T(8,128)(2,1)S(1)} %copy-done.2, f32[256]{0:T(256)S(1)} %multiply_multiply_fusion), kind=kOutput, calls=%fused_computation.3 | convolution fusion | flops 605356032 | bytes 3539968 | tf_op jit(solution)/shard_map/dot_general | solution.py:91
  70.6 0.4 copy-done.22
  72.0 0.4 copy-done.18
  72.8 0.4 copy-done.19
  74.6 24.5 %reduce-scatter.7.cloned.1.call-done = bf16[384,768]{1,0:T(8,128)(2,1)} async-done(((bf16[1536,768]{1,0:T(8,128)(2,1)}), bf16[384,768]{1,0:T(8,128)(2,1)}) %reduce-scatter.7.cloned.1.call-update) | async-done | bytes 589840
  99.1 1.4 copy.37
  100.5 1.1 convert_element_type.140
  102.3 0.8 copy.28
  103.1 1.1 fusion.21
  104.2 1.1 fusion.23
  105.3 1.1 fusion.25
  106.5 1.1 fusion.27
  107.6 1.1 fusion.29
  108.7 1.1 fusion.31
  109.8 0.9 copy.27
  110.8 1.7 convolution_convert_fusion.1
  112.4 55.3 %reduce-scatter.5.cloned.1.call-done = f32[96,384]{1,0:T(8,128)} async-done(((f32[768,384]{1,0:T(8,128)}), f32[96,384]{1,0:T(8,128)}) %reduce-scatter.5.cloned.1.call-update) | async-done | bytes 147472 | tf_op jit(solution)/shard_map/reduce_scatter | solution.py:101
  (137 shorter events, 5.3 us)
Async XLA Ops:
  7.2 49.3 %copy-start.28 = (bf16[256,256]{1,0:T(8,128)(2,1)S(1)}, bf16[256,256]{1,0:T(8,128)(2,1)}, u32[]{:S(2)}) copy-start(bf16[256,256]{1,0:T(8,128)(2,1)} %param.8) | copy-start | bytes 393220
  7.2 49.3 %copy-start.3 = (bf16[256,768]{1,0:T(8,128)(2,1)S(1)}, bf16[256,768]{1,0:T(8,128)(2,1)}, u32[]{:S(2)}) copy-start(bf16[256,768]{1,0:T(8,128)(2,1)} %param.7) | copy-start | bytes 1179652
  7.2 49.3 %copy-start.51 = (s32[256]{0:T(256)S(1)}, s32[256]{0:T(256)}, u32[]{:S(2)}) copy-start(s32[256]{0:T(256)} %param.9) | copy-start | bytes 3076
  7.2 59.0 %all-gather.2.cloned.1.call-start = ((), (), s32[]{:S(2)}) async-start(), calls=%async_computation.2 | async-start | bytes 2949120 | tf_op jit(solution)/shard_map/all_gather | solution.py:83
  7.9 91.1 %reduce-scatter.7.cloned.1.call-start = ((), (), s32[]{:S(2)}) async-start(), calls=%async_computation.4 | async-start | bytes 2949120
  9.1 49.3 %copy-start.15 = (f32[256,256]{0,1:T(8,128)}, f32[256,256]{0,1:T(8,128)S(1)}, u32[]{:S(2)}) copy-start(f32[256,256]{0,1:T(8,128)S(1)} %get-tuple-element.23) | copy-start | bytes 786436
  9.1 49.3 %copy-start.42 = (f32[256]{0:T(256)}, f32[256]{0:T(256)S(1)}, u32[]{:S(2)}) copy-start(f32[256]{0:T(256)S(1)} %get-tuple-element.22) | copy-start | bytes 3076
  9.1 48.3 %copy-start.31 = (s32[256]{0:T(256)S(1)}, s32[256]{0:T(256)}, u32[]{:S(2)}) copy-start(s32[256]{0:T(256)} %param.10) | copy-start | bytes 3076
  9.1 48.3 %copy-start.50 = (s32[256]{0:T(256)S(1)}, s32[256]{0:T(256)}, u32[]{:S(2)}) copy-start(s32[256]{0:T(256)} %param.11) | copy-start | bytes 3076
  10.3 48.9 %copy-start.13 = (f32[256,256]{0,1:T(8,128)}, f32[256,256]{0,1:T(8,128)S(1)}, u32[]{:S(2)}) copy-start(f32[256,256]{0,1:T(8,128)S(1)} %get-tuple-element.27) | copy-start | bytes 786436
  10.3 48.9 %copy-start.40 = (f32[256]{0:T(256)}, f32[256]{0:T(256)S(1)}, u32[]{:S(2)}) copy-start(f32[256]{0:T(256)S(1)} %get-tuple-element.26) | copy-start | bytes 3076
  11.5 48.6 %copy-start.11 = (f32[256,256]{0,1:T(8,128)}, f32[256,256]{0,1:T(8,128)S(1)}, u32[]{:S(2)}) copy-start(f32[256,256]{0,1:T(8,128)S(1)} %get-tuple-element.31) | copy-start | bytes 786436
  11.5 48.6 %copy-start.38 = (f32[256]{0:T(256)}, f32[256]{0:T(256)S(1)}, u32[]{:S(2)}) copy-start(f32[256]{0:T(256)S(1)} %get-tuple-element.30) | copy-start | bytes 3076
  13.0 46.2 %copy-start.44 = (f32[256]{0:T(256)}, f32[256]{0:T(256)S(1)}, u32[]{:S(2)}) copy-start(f32[256]{0:T(256)S(1)} %fusion.37) | copy-start | bytes 3076
  56.5 3.6 %copy-start.46 = (f32[256]{0:T(256)}, f32[256]{0:T(256)S(1)}, u32[]{:S(2)}) copy-start(f32[256]{0:T(256)S(1)} %fusion.41) | copy-start | bytes 3076
  56.7 4.2 %copy-start.6 = (f32[256,256]{0,1:T(8,128)}, f32[256,256]{0,1:T(8,128)S(1)}, u32[]{:S(2)}) copy-start(f32[256,256]{0,1:T(8,128)S(1)} %get-tuple-element.35) | copy-start | bytes 786436
  56.8 4.1 %copy-start.34 = (f32[256]{0:T(256)}, f32[256]{0:T(256)S(1)}, u32[]{:S(2)}) copy-start(f32[256]{0:T(256)S(1)} %fusion.43) | copy-start | bytes 3076
  57.0 4.8 %copy-start.8 = (f32[256,256]{0,1:T(8,128)}, f32[256,256]{0,1:T(8,128)S(1)}, u32[]{:S(2)}) copy-start(f32[256,256]{0,1:T(8,128)S(1)} %get-tuple-element.39) | copy-start | bytes 786436
  57.1 4.8 %copy-start.32 = (f32[256]{0:T(256)}, f32[256]{0:T(256)S(1)}, u32[]{:S(2)}) copy-start(f32[256]{0:T(256)S(1)} %get-tuple-element.38) | copy-start | bytes 3076
  57.1 4.7 %copy-start.36 = (f32[256]{0:T(256)}, f32[256]{0:T(256)S(1)}, u32[]{:S(2)}) copy-start(f32[256]{0:T(256)S(1)} %fusion.45) | copy-start | bytes 3076
  66.1 3.7 %copy-start.5 = (bf16[256,128]{0,1:T(8,128)(2,1)S(1)}, bf16[256,128]{0,1:T(8,128)(2,1)}, u32[]{:S(2)}) copy-start(bf16[256,128]{0,1:T(8,128)(2,1)} %get-tuple-element.21) | copy-start | bytes 196612
  66.1 3.7 %copy-start.23 = (bf16[256,128]{0,1:T(8,128)(2,1)S(1)}, bf16[256,128]{0,1:T(8,128)(2,1)}, u32[]{:S(2)}) copy-start(bf16[256,128]{0,1:T(8,128)(2,1)} %get-tuple-element.25) | copy-start | bytes 196612
  66.1 3.7 %copy-start.24 = (bf16[256,128]{0,1:T(8,128)(2,1)S(1)}, bf16[256,128]{0,1:T(8,128)(2,1)}, u32[]{:S(2)}) copy-start(bf16[256,128]{0,1:T(8,128)(2,1)} %get-tuple-element.29) | copy-start | bytes 196612
  66.1 3.7 %copy-start.25 = (bf16[256,128]{0,1:T(8,128)(2,1)S(1)}, bf16[256,128]{0,1:T(8,128)(2,1)}, u32[]{:S(2)}) copy-start(bf16[256,128]{0,1:T(8,128)(2,1)} %get-tuple-element.33) | copy-start | bytes 196612
  66.1 3.7 %copy-start.26 = (bf16[256,128]{0,1:T(8,128)(2,1)S(1)}, bf16[256,128]{0,1:T(8,128)(2,1)}, u32[]{:S(2)}) copy-start(bf16[256,128]{0,1:T(8,128)(2,1)} %get-tuple-element.37) | copy-start | bytes 196612
  66.1 3.7 %copy-start.27 = (bf16[256,128]{0,1:T(8,128)(2,1)S(1)}, bf16[256,128]{0,1:T(8,128)(2,1)}, u32[]{:S(2)}) copy-start(bf16[256,128]{0,1:T(8,128)(2,1)} %get-tuple-element.41) | copy-start | bytes 196612
  66.1 4.1 %copy-start.29 = (bf16[256,256]{1,0:T(8,128)(2,1)S(1)}, bf16[256,256]{1,0:T(8,128)(2,1)}, u32[]{:S(2)}) copy-start(bf16[256,256]{1,0:T(8,128)(2,1)} %param.8) | copy-start | bytes 393220
  66.1 4.3 %copy-start.4 = (bf16[256,768]{1,0:T(8,128)(2,1)S(1)}, bf16[256,768]{1,0:T(8,128)(2,1)}, u32[]{:S(2)}) copy-start(bf16[256,768]{1,0:T(8,128)(2,1)} %param.7) | copy-start | bytes 1179652
  66.1 101.6 %reduce-scatter.5.cloned.1.call-start = ((), (), s32[]{:S(2)}) async-start(), calls=%async_computation.3 | async-start | bytes 1327104 | tf_op jit(solution)/shard_map/reduce_scatter | solution.py:101
  71.3 30.3 %copy-start.17 = (bf16[256,256]{0,1:T(8,128)(2,1)}, bf16[256,256]{0,1:T(8,128)(2,1)S(1)}, u32[]{:S(2)}) copy-start(bf16[256,256]{0,1:T(8,128)(2,1)S(1)} %fusion.13) | copy-start | bytes 393220
  73.9 27.7 %copy-start.21 = (bf16[256,256]{0,1:T(8,128)(2,1)}, bf16[256,256]{0,1:T(8,128)(2,1)S(1)}, u32[]{:S(2)}) copy-start(bf16[256,256]{0,1:T(8,128)(2,1)S(1)} %fusion.17) | copy-start | bytes 393220
  102.1 8.7 %copy-start = (bf16[768,1536]{1,0:T(8,128)(2,1)S(1)}, bf16[768,1536]{1,0:T(8,128)(2,1)}, u32[]{:S(2)}) copy-start(bf16[768,1536]{1,0:T(8,128)(2,1)} %all-gather.2.cloned.1.call-done) | copy-start | bytes 7077892
  (23 other events, 40.7 us)
Sparse Core Ops, SparseCore 0:
  9.6 27.2 all-gather.1
  66.2 32.8 reduce-scatter.6
  103.1 64.6 reduce-scatter.4
where the time goes:
time: 175 us; the launch traced here: 174 us
  waiting for transfers between devices  80.5 us (46%)
  blocking collectives  42.7 us (24%)
  matrix products  24.7 us (14%)
  between operations  15.2 us (9%)
  local copies, waits for them, and re-layouts  7.96 us (5%)
  other arithmetic  3.1 us (2%)
    reduce_scatter x1, waiting for transfers between devices, on_device(): lax.psum_scatter(column_sums, 'dp', scatter_dimension=0, tiled=True)  55.3 us
    psum x1, blocking collectives, on_device(): resp_total = lax.psum(jnp.sum(in_resp), ('dp', 'fsdp'))  42.7 us
    unnamed x4, waiting for transfers between devices  25.2 us
    unnamed x108, local copies, waits for them, and re-layouts  7.96 us
    dot_general x6, matrix products, attend_backward(): jnp.dot(d_score, keys, preferred_element_type=jnp.float32) * scale  6.73 us
    dot_general x6, matrix products, attend_forward(): jnp.dot(prob.astype(jnp.bfloat16), values, preferred_element_type=jnp.flo...  5.1 us
    dot_general x6, matrix products, attend_forward(): lax.dot_general(q_head, keys, (((1,), (1,)), ((), ())), preferred_element...  4.15 us
  transfers between devices with their start and end apart: 3, of which 2 were waited for; matrix products, arithmetic and copies ran while one was open for 18% of the time, Pallas kernels for 0%

commit v1 on v0

--- a/solution.py
+++ b/solution.py
@@ -1,9 +1,365 @@
+import functools
+
 import jax
 import jax.numpy as jnp
 from jax import lax
+from jax.experimental import pallas as pl
+from jax.experimental.pallas import tpu as pltpu
 from jax.sharding import PartitionSpec as P
 
+MESH = pl.DeviceIdType.MESH
 neg_fill = -1e30
+bf16 = jnp.bfloat16
+f32 = jnp.float32
+W_CHUNKS = 3
+
+
+def dot(a, b, dims):
+    return lax.dot_general(a, b, ((dims[0], dims[1]), ((), ())), preferred_element_type=f32)
+
+
+def fused_kernel(
+    sizes,
+    q_hbm, kv_hbm, seg_hbm, resp_hbm, adv_hbm, w_hbm, up_hbm,
+    bo_hbm, gq_hbm, gkv_hbm, gw_hbm,
+    q, kv, seg, resp, adv, up,
+    w_all, d_out, bo, attn, prob, d_attn, bias, cnt, gq, gkv, gw,
+    part, c_recv, x_send, x_recv, z_send, z_recv, y_send, y_recv,
+    cnt_y, cnt_z,
+    load_sem, out_sem, bo_sem,
+    ws_sem, wr_sem, cs_sem, cr_sem, xs_sem, xr_sem, zs_sem, zr_sem, ys_sem, yr_sem,
+    ns_sem, nr_sem, nys_sem, nyr_sem, nzs_sem, nzr_sem,
+):
+    nd, nf, tok, heads, head, rows, cols = sizes
+    nz, ny = nd // 2, nf // 2
+    half_heads, half_blocks = heads // 2, nd // 2
+    scale = head ** (-0.5)
+    dp, fs = lax.axis_index("dp"), lax.axis_index("fsdp")
+    c, y = lax.rem(fs, 2), lax.div(fs, 2)
+    x, z = lax.rem(dp, 2), lax.div(dp, 2)
+    sib_f = y * 2 + 1 - c
+    sib = (dp, sib_f)
+    x_peer = (z * 2 + 1 - x, fs)
+
+    def y_of(j):
+        return lax.rem(y + j, ny)
+
+    def z_of(k):
+        return lax.rem(z + k, nz)
+
+    def y_dev(j):
+        return (dp, y_of(j) * 2 + c)
+
+    def z_dev(k):
+        return (z_of(k) * 2 + x, fs)
+
+    def remote(src, dst, ss, rs, dev):
+        return pltpu.make_async_remote_copy(
+            src_ref=src, dst_ref=dst, send_sem=ss, recv_sem=rs, device_id=dev, device_id_type=MESH
+        )
+
+    sends = []
+
+    def send(*args):
+        copy = remote(*args)
+        copy.start()
+        sends.append(copy)
+
+    loads = [
+        pltpu.make_async_copy(a, b, load_sem.at[i])
+        for i, (a, b) in enumerate(
+            [(seg_hbm, seg), (resp_hbm, resp), (adv_hbm, adv), (q_hbm, q), (kv_hbm, kv),
+             (up_hbm, up), (w_hbm, w_all.at[fs])]
+        )
+    ]
+    for load in loads:
+        load.start()
+
+    barrier = pltpu.get_barrier_semaphore()
+    peers = [sib, x_peer] + [y_dev(j) for j in range(1, ny)] + [z_dev(k) for k in range(1, nz)]
+    for peer in peers:
+        pl.semaphore_signal(barrier, inc=1, device_id=peer, device_id_type=MESH)
+    pl.semaphore_wait(barrier, len(peers))
+
+    depth = heads * head
+    step = depth // W_CHUNKS
+
+    def w_rows(i):
+        return pl.ds(i * step, step)
+
+    for i in range(W_CHUNKS):
+        for j in range(1, ny):
+            send(w_hbm.at[w_rows(i)], w_all.at[fs, w_rows(i)], ws_sem.at[j, i], wr_sem.at[fs, i], y_dev(j))
+    for i in range(W_CHUNKS):
+        send(w_hbm.at[w_rows(i)], w_all.at[fs, w_rows(i)], ws_sem.at[0, i], wr_sem.at[fs, i], sib)
+
+    def w_wait(shard, i):
+        ref = w_all.at[shard, w_rows(i)]
+        remote(ref, ref, ws_sem.at[0, i], wr_sem.at[shard, i], sib).wait_recv()
+
+    def w_forward(i):
+        for j in range(1, ny):
+            shard = y_of(j) * 2 + c
+            w_wait(shard, i)
+            send(w_all.at[shard, w_rows(i)], w_all.at[shard, w_rows(i)],
+                 ws_sem.at[ny - 1 + j, i], wr_sem.at[shard, i], sib)
+
+    for load in loads[:3]:
+        load.wait()
+    count = jnp.sum(resp[...].astype(f32), axis=1, keepdims=True)
+    cnt[0] = jnp.broadcast_to(count, cnt.shape[1:])
+    coef_row = resp[...].astype(f32) * (adv[...].astype(f32) * 0.125)
+    coef = jnp.transpose(jnp.broadcast_to(coef_row, (128, tok)))[:, :1]
+    seg_k = jnp.broadcast_to(seg[...].astype(f32), (tok, tok))
+    seg_q = jnp.transpose(seg_k)
+    at_q = lax.broadcasted_iota(jnp.int32, (tok, tok), 0)
+    at_k = lax.broadcasted_iota(jnp.int32, (tok, tok), 1)
+    bias[...] = jnp.where((seg_q == seg_k) & (at_k <= at_q), 0.0, neg_fill)
+    send(cnt.at[0], cnt.at[1], ns_sem.at[0], nr_sem.at[0], sib)
+    for load in loads[3:6]:
+        load.wait()
+    for s in range(nf):
+        d_out[s] = (coef * up[:, s * cols:(s + 1) * cols].astype(f32)).astype(bf16)
+    keys, values = kv[:, :head], kv[:, head:]
+
+    def forward(h):
+        cut = slice(h * head, (h + 1) * head)
+        scores = dot(q[:, cut], keys, ((1,), (1,))) * scale + bias[...]
+        top = jnp.max(scores, axis=1, keepdims=True)
+        expo = jnp.exp(scores - top)
+        p = (expo * (1.0 / jnp.sum(expo, axis=1, keepdims=True))).astype(bf16)
+        prob[h] = p
+        attn[:, cut] = dot(p, values, ((1,), (0,))).astype(bf16)
+
+    def partial(hf):
+        width = half_heads * head
+        left = attn[:, hf * width:(hf + 1) * width]
+        for s in range(nf):
+            got = dot(left, d_out[s], ((0,), (0,))).astype(bf16)
+            for b in range(half_blocks):
+                part[s, hf * half_blocks + b] = got[b * rows:(b + 1) * rows]
+        blocks = pl.ds(hf * half_blocks, half_blocks)
+        for j in range(1, ny + 1):
+            yy = y_of(j)
+            send(part.at[yy * 2 + 1 - c, blocks], c_recv.at[yy, blocks],
+                 cs_sem.at[hf, yy], cr_sem.at[hf, yy], sib)
+
+    def c_stage(hf):
+        blocks = pl.ds(hf * half_blocks, half_blocks)
+        for j in range(1, ny + 1):
+            yy = y_of(j)
+            ref = c_recv.at[yy, blocks]
+            remote(ref, ref, cs_sem.at[hf, yy], cr_sem.at[hf, yy], sib).wait_recv()
+            for zz in range(hf * nz // 2, (hf + 1) * nz // 2):
+                block = zz * 2 + 1 - x
+                both = part[yy * 2 + c, block].astype(f32) + c_recv[yy, block].astype(f32)
+                x_send[zz, yy] = both.astype(bf16)
+                send(x_send.at[zz, yy], x_recv.at[zz, yy], xs_sem.at[zz, yy], xr_sem.at[zz, yy], x_peer)
+
+    def x_stage(zz, j):
+        yy = y_of(j)
+        ref = x_recv.at[zz, yy]
+        remote(ref, ref, xs_sem.at[zz, yy], xr_sem.at[zz, yy], x_peer).wait_recv()
+        block = zz * 2 + x
+        total = part[yy * 2 + c, block].astype(f32) + c_recv[yy, block].astype(f32) + ref[...].astype(f32)
+        z_send[zz, yy] = total.astype(bf16)
+
+        @pl.when(zz != z)
+        def _():
+            remote(z_send.at[zz, yy], z_recv.at[z, yy], zs_sem.at[zz, yy], zr_sem.at[z, yy],
+                   (zz * 2 + x, fs)).start()
+
+    def z_stage(j):
+        yy = y_of(j)
+        total = z_send[z, yy].astype(f32)
+        for k in range(1, nz):
+            src = z_of(k)
+            ref = z_recv.at[src, yy]
+            remote(ref, ref, zs_sem.at[src, yy], zr_sem.at[src, yy], z_dev(k)).wait_recv()
+            total = total + ref[...].astype(f32)
+        return total
+
+    def use_weight(s, first=False):
+        w = w_all[s]
+        bo[s] = dot(attn[...], w, ((1,), (0,))).astype(bf16)
+        pltpu.make_async_copy(
+            bo.at[s], bo_hbm.at[:, pl.ds(pl.multiple_of(s * cols, 128), cols)], bo_sem.at[s]
+        ).start()
+        grad = dot(d_out[s], w, ((1,), (1,)))
+        d_attn[...] = grad if first else d_attn[...] + grad
+
+    def count_core():
+        remote(cnt.at[1], cnt.at[1], ns_sem.at[0], nr_sem.at[0], sib).wait_recv()
+        cnt[2] = cnt[0] + cnt[1]
+        for j in range(1, ny):
+            send(cnt.at[2], cnt_y.at[y], nys_sem.at[j], nyr_sem.at[y], y_dev(j))
+
+    def count_y():
+        total = cnt[2]
+        for j in range(1, ny):
+            ref = cnt_y.at[y_of(j)]
+            remote(ref, ref, nys_sem.at[j], nyr_sem.at[y_of(j)], y_dev(j)).wait_recv()
+            total = total + ref[...]
+        cnt[3] = total
+        send(cnt.at[3], cnt.at[4], ns_sem.at[1], nr_sem.at[1], x_peer)
+
+    def count_x():
+        remote(cnt.at[4], cnt.at[4], ns_sem.at[1], nr_sem.at[1], x_peer).wait_recv()
+        cnt[5] = cnt[3] + cnt[4]
+        for k in range(1, nz):
+            send(cnt.at[5], cnt_z.at[z], nzs_sem.at[k], nzr_sem.at[z], z_dev(k))
+
+    def count_z():
+        total = cnt[5]
+        for k in range(1, nz):
+            ref = cnt_z.at[z_of(k)]
+            remote(ref, ref, nzs_sem.at[k], nzr_sem.at[z_of(k)], z_dev(k)).wait_recv()
+            total = total + ref[...]
+        return -(f32(tok * nd * nf) / total[:1, :1])
+
+    for h in range(half_heads):
+        forward(h)
+    partial(0)
+    for h in range(half_heads, heads):
+        forward(h)
+    count_core()
+    partial(1)
+    c_stage(0)
+    count_y()
+    loads[6].wait()
+    c_stage(1)
+    use_weight(fs, first=True)
+    w_forward(0)
+    for i in range(W_CHUNKS):
+        w_wait(sib_f, i)
+    use_weight(sib_f)
+    count_x()
+
+    state = {}
+
+    def weights_of(j):
+        shard = y_of(j) * 2 + c
+        use_weight(shard)
+
+    def weights_other(j):
+        shard = y_of(j) * 2 + 1 - c
+        for i in range(W_CHUNKS):
+            w_wait(shard, i)
+        use_weight(shard)
+
+    def backward(h):
+        if h == 0:
+            state["factor"] = count_z()
+            state["gk"] = jnp.zeros((tok, head), f32)
+            state["gv"] = jnp.zeros((tok, head), f32)
+        factor = state["factor"]
+        cut = slice(h * head, (h + 1) * head)
+        d_full = d_attn[:, cut]
+        d_head = d_full.astype(bf16)
+        delta = jnp.sum(d_head.astype(f32) * attn[:, cut].astype(f32), axis=1, keepdims=True)
+        p = prob[h]
+        d_prob = dot(d_head, values, ((1,), (1,)))
+        d_score = (p.astype(f32) * (d_prob - delta)).astype(bf16)
+        gq[:, cut] = (dot(d_score, keys, ((1,), (0,))) * (scale * factor)).astype(bf16)
+        state["gk"] = state["gk"] + dot(d_score, q[:, cut], ((0,), (0,)))
+        state["gv"] = state["gv"] + dot(p, d_head, ((0,), (0,)))
+        if h == heads - 1:
+            gkv[:, :head] = (state["gk"] * (scale * factor)).astype(bf16)
+            gkv[:, head:] = (state["gv"] * factor).astype(bf16)
+            pltpu.make_async_copy(gq, gq_hbm, out_sem.at[0]).start()
+            pltpu.make_async_copy(gkv, gkv_hbm, out_sem.at[1]).start()
+
+    x_steps = [
+        functools.partial(x_stage, zz, j)
+        for hf in range(2)
+        for j in range(1, ny + 1)
+        for zz in range(hf * nz // 2, (hf + 1) * nz // 2)
+    ]
+    fillers = [functools.partial(w_forward, i) for i in range(1, W_CHUNKS)]
+    fillers += [functools.partial(weights_of, j) for j in range(1, ny)]
+    fillers += [functools.partial(weights_other, j) for j in range(1, ny)]
+    fillers += [functools.partial(backward, h) for h in range(heads)]
+    done = 0
+    for n, x_step in enumerate(x_steps):
+        x_step()
+        until = (n + 1) * len(fillers) // len(x_steps)
+        for filler in fillers[done:until]:
+            filler()
+        done = until
+
+    factor = state["factor"]
+    for j in range(1, ny):
+        y_send[j - 1] = z_stage(j).astype(bf16)
+        send(y_send.at[j - 1], y_recv.at[y], ys_sem.at[j - 1], yr_sem.at[y], y_dev(j))
+    total = z_stage(ny)
+    for j in range(1, ny):
+        src = y_of(j)
+        ref = y_recv.at[src]
+        remote(ref, ref, ys_sem.at[j - 1], yr_sem.at[src], y_dev(j)).wait_recv()
+        total = total + ref[...].astype(f32)
+    gw[...] = total * factor
+    pltpu.make_async_copy(gw, gw_hbm, out_sem.at[2]).start()
+
+    for copy in sends:
+        copy.wait_send()
+    for zz in range(nz):
+        for yy in range(ny):
+            @pl.when(zz != z)
+            def _(zz=zz, yy=yy):
+                remote(z_send.at[zz, yy], z_recv.at[z, yy], zs_sem.at[zz, yy], zr_sem.at[z, yy],
+                       (zz * 2 + x, fs)).wait_send()
+    for s in range(nf):
+        pltpu.make_async_copy(bo.at[s], bo_hbm.at[:, pl.ds(s * cols, cols)], bo_sem.at[s]).wait()
+    pltpu.make_async_copy(gq, gq_hbm, out_sem.at[0]).wait()
+    pltpu.make_async_copy(gkv, gkv_hbm, out_sem.at[1]).wait()
+    pltpu.make_async_copy(gw, gw_hbm, out_sem.at[2]).wait()
+
+
+def fused(nd, nf, queries, keys_values, seg_ids, in_resp, advantage, out_weight, upstream):
+    tok, depth = queries.shape
+    head = keys_values.shape[1] // 2
+    heads = depth // head
+    cols = out_weight.shape[1]
+    rows = depth // nd
+    nz, ny = nd // 2, nf // 2
+    any_spec = pl.BlockSpec(memory_space=pl.ANY)
+    V, D = pltpu.VMEM, pltpu.SemaphoreType.DMA
+    return pl.pallas_call(
+        functools.partial(fused_kernel, (nd, nf, tok, heads, head, rows, cols)),
+        out_shape=(
+            jax.ShapeDtypeStruct((tok, nf * cols), bf16),
+            jax.ShapeDtypeStruct((tok, depth), bf16),
+            jax.ShapeDtypeStruct((tok, 2 * head), bf16),
+            jax.ShapeDtypeStruct((rows, cols), f32),
+        ),
+        in_specs=[any_spec] * 7,
+        out_specs=(any_spec,) * 4,
+        scratch_shapes=[
+            V((tok, depth), bf16), V((tok, 2 * head), bf16),
+            V((1, tok), jnp.int32), V((1, tok), jnp.int32), V((1, tok), jnp.int32),
+            V((tok, nf * cols), bf16),
+            V((nf, depth, cols), bf16), V((nf, tok, cols), bf16), V((nf, tok, cols), bf16),
+            V((tok, depth), bf16), V((heads, tok, tok), bf16), V((tok, depth), f32),
+            V((tok, tok), f32), V((6, 8, 128), f32),
+            V((tok, depth), bf16), V((tok, 2 * head), bf16), V((rows, cols), f32),
+            V((nf, nd, rows, cols), bf16), V((ny, nd, rows, cols), bf16),
+            V((nz, ny, rows, cols), bf16), V((nz, ny, rows, cols), bf16),
+            V((nz, ny, rows, cols), bf16), V((nz, ny, rows, cols), bf16),
+            V((ny, rows, cols), bf16), V((ny, rows, cols), bf16),
+            V((ny, 8, 128), f32), V((nz, 8, 128), f32),
+            D((7,)), D((3,)), D((nf,)),
+            D((nf, W_CHUNKS)), D((nf, W_CHUNKS)),
+            D((2, ny)), D((2, ny)), D((nz, ny)), D((nz, ny)), D((nz, ny)), D((nz, ny)),
+            D((ny,)), D((ny,)),
+            D((2,)), D((2,)), D((ny,)), D((ny,)), D((nz,)), D((nz,)),
+        ],
+        compiler_params=pltpu.CompilerParams(
+            collective_id=0, has_side_effects=True, vmem_limit_bytes=48 * 1024 * 1024
+        ),
+    )(
+        queries, keys_values, seg_ids.reshape(1, -1), in_resp.reshape(1, -1),
+        advantage.reshape(1, -1), out_weight, upstream,
+    )
 
 
 def attend_forward(q_rows, kv_rows, seg_rows):
@@ -119,6 +475,21 @@
         P(("dp", "fsdp"), None),
         P("dp", "fsdp"),
     )
+    nd, nf = mesh.shape["dp"], mesh.shape["fsdp"]
+
+    def on_each(queries, keys_values, seg_ids, in_resp, advantage, out_weight, upstream):
+        args = (queries, keys_values, seg_ids, in_resp, advantage, out_weight, upstream)
+        depth, cols = out_weight.shape
+        head = keys_values.shape[1] // 2
+        heads = depth // head
+        fits = (
+            nd % 4 == 0 and nf % 2 == 0 and heads % 2 == 0 and depth % (16 * nd) == 0
+            and cols % 128 == 0 and head % 128 == 0 and depth % (16 * W_CHUNKS) == 0
+        )
+        if fits:
+            return fused(nd, nf, *args)
+        return on_device(*args)
+
     return jax.shard_map(
-        on_device, mesh=mesh, in_specs=in_specs, out_specs=out_specs, check_vma=False
-    )
+        on_each, mesh=mesh, in_specs=in_specs, out_specs=out_specs, check_vma=False
+    )

time: 175 us -> 48.4 us (0.28)
  the two profiles are of different devices: /device:TPU:0 before, /device:TPU:24 now
where the time goes in v1:
time: 48.4 us; the launch traced here: 48.1 us
  Pallas kernels  39.7 us (82%)
  local copies, waits for them, and re-layouts  7.72 us (16%)
  between operations  0.67 us (1%)
    pallas_call x1, Pallas kernels, fused(): pl.pallas_call(functools.partial(fused_kernel, (nd, nf, tok, heads, head,...  39.7 us
    unnamed x18, local copies, waits for them, and re-layouts  7.72 us

profile of v1, /device:TPU:24, one launch (start us, length us, event | category | flops | bytes accessed | tf_op | source)
XLA Modules:
  0.0 48.1 jit_solution(3734825938661529663)
XLA Ops:
  0.6 0.0 copy-start.5
  0.6 0.0 copy-start.6
  0.7 0.0 copy-start.4
  0.7 0.7 %copy-done.5 = s32[256]{0:T(256)S(1)} copy-done((s32[256]{0:T(256)S(1)}, s32[256]{0:T(256)}, u32[]{:S(2)}) %copy-start.5) | copy-done | bytes 1048
  1.3 0.0 copy-done.6
  1.3 0.0 copy-done.4
  1.3 0.0 copy-start
  1.3 1.1 %copy-done = bf16[256,1536]{1,0:T(8,128)(2,1)S(1)} copy-done((bf16[256,1536]{1,0:T(8,128)(2,1)S(1)}, bf16[256,1536]{1,0:T(8,128)(2,1)}, u32[]{:S(2)}) %copy-start) | copy-done | bytes 786456
  2.5 0.0 copy-start.1
  2.5 1.1 %copy-done.1 = bf16[768,384]{1,0:T(8,128)(2,1)S(1)} copy-done((bf16[768,384]{1,0:T(8,128)(2,1)S(1)}, bf16[768,384]{1,0:T(8,128)(2,1)}, u32[]{:S(2)}) %copy-start.1) | copy-done | bytes 589848
  3.5 0.0 copy-start.2
  3.5 1.0 %copy-done.2 = bf16[256,768]{1,0:T(8,128)(2,1)S(1)} copy-done((bf16[256,768]{1,0:T(8,128)(2,1)S(1)}, bf16[256,768]{1,0:T(8,128)(2,1)}, u32[]{:S(2)}) %copy-start.2) | copy-done | bytes 393240
  4.5 0.0 copy-start.3
  4.5 0.9 %copy-done.3 = bf16[256,256]{1,0:T(8,128)(2,1)S(1)} copy-done((bf16[256,256]{1,0:T(8,128)(2,1)S(1)}, bf16[256,256]{1,0:T(8,128)(2,1)}, u32[]{:S(2)}) %copy-start.3) | copy-done | bytes 131096
  5.4 39.7 %shard_map.102 = (bf16[256,1536]{1,0:T(8,128)(2,1)S(1)}, bf16[256,768]{1,0:T(8,128)(2,1)S(1)}, bf16[256,256]{1,0:T(8,128)(2,1)S(1)}, f32[96,384]{1,0:T(8,128)S(1)}) custom-call(bf16[256,768]{1,0:T(8,128)(2,1)S(1)} %copy-done.2, bf16[256,256]{1,0:T(8,128)(2,1)S(1)} %copy-done.3, s32[1,256]{1,0:T(1,128)S(1)} %bitcast.3, s32[1,256]{1,0:T(1,128)S(1)} %bitcast.4, ...), custom_call_target="tpu_custom_call" | custom-call | tf_op jit(solution)/shard_map/pallas_call | solution.py:327
  45.1 0.9 %copy.15 = bf16[256,1536]{1,0:T(8,128)(2,1)} copy(bf16[256,1536]{1,0:T(8,128)(2,1)S(1)} %get-tuple-element.8) | data formatting | bytes 1572864
  46.0 0.7 %copy.16 = bf16[256,768]{1,0:T(8,128)(2,1)} copy(bf16[256,768]{1,0:T(8,128)(2,1)S(1)} %get-tuple-element.9) | data formatting | bytes 786432
  46.8 0.7 %copy.17 = bf16[256,256]{1,0:T(8,128)(2,1)} copy(bf16[256,256]{1,0:T(8,128)(2,1)S(1)} %get-tuple-element.10) | data formatting | bytes 262144
  47.4 0.7 %copy.18 = f32[96,384]{1,0:T(8,128)} copy(f32[96,384]{1,0:T(8,128)S(1)} %get-tuple-element.11) | data formatting | bytes 294912
Async XLA Ops:
  0.6 0.7 %copy-start.5 = (s32[256]{0:T(256)S(1)}, s32[256]{0:T(256)}, u32[]{:S(2)}) copy-start(s32[256]{0:T(256)} %param.10) | copy-start | bytes 3076
  0.6 0.7 %copy-start.6 = (s32[256]{0:T(256)S(1)}, s32[256]{0:T(256)}, u32[]{:S(2)}) copy-start(s32[256]{0:T(256)} %param.11) | copy-start | bytes 3076
  0.7 0.7 %copy-start.4 = (s32[256]{0:T(256)S(1)}, s32[256]{0:T(256)}, u32[]{:S(2)}) copy-start(s32[256]{0:T(256)} %param.9) | copy-start | bytes 3076
  1.3 1.1 %copy-start = (bf16[256,1536]{1,0:T(8,128)(2,1)S(1)}, bf16[256,1536]{1,0:T(8,128)(2,1)}, u32[]{:S(2)}) copy-start(bf16[256,1536]{1,0:T(8,128)(2,1)} %up_hbm.1) | copy-start | bytes 2359300
  2.5 1.1 %copy-start.1 = (bf16[768,384]{1,0:T(8,128)(2,1)S(1)}, bf16[768,384]{1,0:T(8,128)(2,1)}, u32[]{:S(2)}) copy-start(bf16[768,384]{1,0:T(8,128)(2,1)} %w_hbm.1) | copy-start | bytes 1769476
  3.5 1.0 %copy-start.2 = (bf16[256,768]{1,0:T(8,128)(2,1)S(1)}, bf16[256,768]{1,0:T(8,128)(2,1)}, u32[]{:S(2)}) copy-start(bf16[256,768]{1,0:T(8,128)(2,1)} %q_hbm.1) | copy-start | bytes 1179652
  4.5 0.9 %copy-start.3 = (bf16[256,256]{1,0:T(8,128)(2,1)S(1)}, bf16[256,256]{1,0:T(8,128)(2,1)}, u32[]{:S(2)}) copy-start(bf16[256,256]{1,0:T(8,128)(2,1)} %kv_hbm.1) | copy-start | bytes 393220

commit v2 on v1

--- a/solution.py
+++ b/solution.py
@@ -21,18 +21,18 @@
 def fused_kernel(
     sizes,
     q_hbm, kv_hbm, seg_hbm, resp_hbm, adv_hbm, w_hbm, up_hbm,
-    bo_hbm, gq_hbm, gkv_hbm, gw_hbm,
+    bo, gq, gkv, gw,
     q, kv, seg, resp, adv, up,
-    w_all, d_out, bo, attn, prob, d_attn, bias, cnt, gq, gkv, gw,
+    w_all, d_out, attn, prob, d_attn, bias, cnt,
     part, c_recv, x_send, x_recv, z_send, z_recv, y_send, y_recv,
     cnt_y, cnt_z,
-    load_sem, out_sem, bo_sem,
+    load_sem,
     ws_sem, wr_sem, cs_sem, cr_sem, xs_sem, xr_sem, zs_sem, zr_sem, ys_sem, yr_sem,
     ns_sem, nr_sem, nys_sem, nyr_sem, nzs_sem, nzr_sem,
 ):
     nd, nf, tok, heads, head, rows, cols = sizes
     nz, ny = nd // 2, nf // 2
-    half_heads, half_blocks = heads // 2, nd // 2
+    half_heads, half_blocks, half_z = heads // 2, nd // 2, nz // 2
     scale = head ** (-0.5)
     dp, fs = lax.axis_index("dp"), lax.axis_index("fsdp")
     c, y = lax.rem(fs, 2), lax.div(fs, 2)
@@ -41,6 +41,15 @@
     sib = (dp, sib_f)
     x_peer = (z * 2 + 1 - x, fs)
 
+    far = 1 - lax.div(z, half_z)
+    halves = (far, 1 - far)
+
+    def owners(n):
+        base = halves[n] * half_z
+        if n == 0:
+            return [base + i for i in range(half_z)]
+        return [base + lax.rem(z - base + 1 + i, half_z) for i in range(half_z)]
+
     def y_of(j):
         return lax.rem(y + j, ny)
 
@@ -75,11 +84,17 @@
     for load in loads:
         load.start()
 
+    loads[1].wait()
+    count = jnp.sum(resp[...].astype(f32), axis=1, keepdims=True)
+    cnt[0] = jnp.broadcast_to(count, cnt.shape[1:])
+
     barrier = pltpu.get_barrier_semaphore()
     peers = [sib, x_peer] + [y_dev(j) for j in range(1, ny)] + [z_dev(k) for k in range(1, nz)]
     for peer in peers:
         pl.semaphore_signal(barrier, inc=1, device_id=peer, device_id_type=MESH)
     pl.semaphore_wait(barrier, len(peers))
+    for j in range(1, ny):
+        send(cnt.at[0], cnt_y.at[y], nys_sem.at[j], nyr_sem.at[y], y_dev(j))
 
     depth = heads * head
     step = depth // W_CHUNKS
@@ -104,10 +119,8 @@
             send(w_all.at[shard, w_rows(i)], w_all.at[shard, w_rows(i)],
                  ws_sem.at[ny - 1 + j, i], wr_sem.at[shard, i], sib)
 
-    for load in loads[:3]:
+    for load in (loads[0], loads[2]):
         load.wait()
-    count = jnp.sum(resp[...].astype(f32), axis=1, keepdims=True)
-    cnt[0] = jnp.broadcast_to(count, cnt.shape[1:])
     coef_row = resp[...].astype(f32) * (adv[...].astype(f32) * 0.125)
     coef = jnp.transpose(jnp.broadcast_to(coef_row, (128, tok)))[:, :1]
     seg_k = jnp.broadcast_to(seg[...].astype(f32), (tok, tok))
@@ -115,15 +128,17 @@
     at_q = lax.broadcasted_iota(jnp.int32, (tok, tok), 0)
     at_k = lax.broadcasted_iota(jnp.int32, (tok, tok), 1)
     bias[...] = jnp.where((seg_q == seg_k) & (at_k <= at_q), 0.0, neg_fill)
-    send(cnt.at[0], cnt.at[1], ns_sem.at[0], nr_sem.at[0], sib)
     for load in loads[3:6]:
         load.wait()
     for s in range(nf):
         d_out[s] = (coef * up[:, s * cols:(s + 1) * cols].astype(f32)).astype(bf16)
     keys, values = kv[:, :head], kv[:, head:]
 
+    def lanes(h):
+        return pl.ds(pl.multiple_of(h * head, 128), head)
+
     def forward(h):
-        cut = slice(h * head, (h + 1) * head)
+        cut = lanes(h)
         scores = dot(q[:, cut], keys, ((1,), (1,))) * scale + bias[...]
         top = jnp.max(scores, axis=1, keepdims=True)
         expo = jnp.exp(scores - top)
@@ -131,43 +146,53 @@
         prob[h] = p
         attn[:, cut] = dot(p, values, ((1,), (0,))).astype(bf16)
 
-    def partial(hf):
+    def partial(n):
         width = half_heads * head
-        left = attn[:, hf * width:(hf + 1) * width]
-        for s in range(nf):
+        left = attn[:, pl.ds(pl.multiple_of(halves[n] * width, 128), width)]
+        first = halves[n] * half_blocks
+        blocks = pl.ds(first, half_blocks)
+
+        def shard(s):
             got = dot(left, d_out[s], ((0,), (0,))).astype(bf16)
             for b in range(half_blocks):
-                part[s, hf * half_blocks + b] = got[b * rows:(b + 1) * rows]
-        blocks = pl.ds(hf * half_blocks, half_blocks)
+                part[s, first + b] = got[b * rows:(b + 1) * rows]
+
         for j in range(1, ny + 1):
             yy = y_of(j)
+            shard(yy * 2 + 1 - c)
             send(part.at[yy * 2 + 1 - c, blocks], c_recv.at[yy, blocks],
-                 cs_sem.at[hf, yy], cr_sem.at[hf, yy], sib)
-
-    def c_stage(hf):
-        blocks = pl.ds(hf * half_blocks, half_blocks)
+                 cs_sem.at[n, yy], cr_sem.at[n, yy], sib)
         for j in range(1, ny + 1):
+            shard(y_of(j) * 2 + c)
+
+    def x_order(n):
+        zs = owners(n)
+        return [(zz, j, n == 0 or zz is not zs[-1]) for j in range(1, ny + 1) for zz in zs]
+
+    def c_stage(n):
+        blocks = pl.ds(halves[n] * half_blocks, half_blocks)
+        waited = set()
+        for zz, j, _ in x_order(n):
             yy = y_of(j)
-            ref = c_recv.at[yy, blocks]
-            remote(ref, ref, cs_sem.at[hf, yy], cr_sem.at[hf, yy], sib).wait_recv()
-            for zz in range(hf * nz // 2, (hf + 1) * nz // 2):
-                block = zz * 2 + 1 - x
-                both = part[yy * 2 + c, block].astype(f32) + c_recv[yy, block].astype(f32)
-                x_send[zz, yy] = both.astype(bf16)
-                send(x_send.at[zz, yy], x_recv.at[zz, yy], xs_sem.at[zz, yy], xr_sem.at[zz, yy], x_peer)
-
-    def x_stage(zz, j):
+            if j not in waited:
+                waited.add(j)
+                ref = c_recv.at[yy, blocks]
+                remote(ref, ref, cs_sem.at[n, yy], cr_sem.at[n, yy], sib).wait_recv()
+            block = zz * 2 + 1 - x
+            both = part[yy * 2 + c, block].astype(f32) + c_recv[yy, block].astype(f32)
+            x_send[zz, yy] = both.astype(bf16)
+            send(x_send.at[zz, yy], x_recv.at[zz, yy], xs_sem.at[zz, yy], xr_sem.at[zz, yy], x_peer)
+
+    def x_stage(zz, j, leaves):
         yy = y_of(j)
         ref = x_recv.at[zz, yy]
         remote(ref, ref, xs_sem.at[zz, yy], xr_sem.at[zz, yy], x_peer).wait_recv()
         block = zz * 2 + x
         total = part[yy * 2 + c, block].astype(f32) + c_recv[yy, block].astype(f32) + ref[...].astype(f32)
         z_send[zz, yy] = total.astype(bf16)
-
-        @pl.when(zz != z)
-        def _():
-            remote(z_send.at[zz, yy], z_recv.at[z, yy], zs_sem.at[zz, yy], zr_sem.at[z, yy],
-                   (zz * 2 + x, fs)).start()
+        if leaves:
+            send(z_send.at[zz, yy], z_recv.at[z, yy], zs_sem.at[zz, yy], zr_sem.at[z, yy],
+                 (zz * 2 + x, fs))
 
     def z_stage(j):
         yy = y_of(j)
@@ -181,26 +206,22 @@
 
     def use_weight(s, first=False):
         w = w_all[s]
-        bo[s] = dot(attn[...], w, ((1,), (0,))).astype(bf16)
-        pltpu.make_async_copy(
-            bo.at[s], bo_hbm.at[:, pl.ds(pl.multiple_of(s * cols, 128), cols)], bo_sem.at[s]
-        ).start()
+        bo[:, pl.ds(pl.multiple_of(s * cols, 128), cols)] = dot(attn[...], w, ((1,), (0,))).astype(bf16)
         grad = dot(d_out[s], w, ((1,), (1,)))
         d_attn[...] = grad if first else d_attn[...] + grad
 
-    def count_core():
-        remote(cnt.at[1], cnt.at[1], ns_sem.at[0], nr_sem.at[0], sib).wait_recv()
-        cnt[2] = cnt[0] + cnt[1]
-        for j in range(1, ny):
-            send(cnt.at[2], cnt_y.at[y], nys_sem.at[j], nyr_sem.at[y], y_dev(j))
-
     def count_y():
-        total = cnt[2]
+        total = cnt[0]
         for j in range(1, ny):
             ref = cnt_y.at[y_of(j)]
             remote(ref, ref, nys_sem.at[j], nyr_sem.at[y_of(j)], y_dev(j)).wait_recv()
             total = total + ref[...]
-        cnt[3] = total
+        cnt[1] = total
+        send(cnt.at[1], cnt.at[2], ns_sem.at[0], nr_sem.at[0], sib)
+
+    def count_core():
+        remote(cnt.at[2], cnt.at[2], ns_sem.at[0], nr_sem.at[0], sib).wait_recv()
+        cnt[3] = cnt[1] + cnt[2]
         send(cnt.at[3], cnt.at[4], ns_sem.at[1], nr_sem.at[1], x_peer)
 
     def count_x():
@@ -217,23 +238,23 @@
             total = total + ref[...]
         return -(f32(tok * nd * nf) / total[:1, :1])
 
-    for h in range(half_heads):
-        forward(h)
+    for i in range(half_heads):
+        forward(halves[0] * half_heads + i)
+    count_y()
     partial(0)
-    for h in range(half_heads, heads):
-        forward(h)
     count_core()
+    for i in range(half_heads):
+        forward(halves[1] * half_heads + i)
+    c_stage(0)
     partial(1)
-    c_stage(0)
-    count_y()
+    count_x()
+    c_stage(1)
     loads[6].wait()
-    c_stage(1)
     use_weight(fs, first=True)
     w_forward(0)
     for i in range(W_CHUNKS):
         w_wait(sib_f, i)
     use_weight(sib_f)
-    count_x()
 
     state = {}
 
@@ -266,31 +287,27 @@
         if h == heads - 1:
             gkv[:, :head] = (state["gk"] * (scale * factor)).astype(bf16)
             gkv[:, head:] = (state["gv"] * factor).astype(bf16)
-            pltpu.make_async_copy(gq, gq_hbm, out_sem.at[0]).start()
-            pltpu.make_async_copy(gkv, gkv_hbm, out_sem.at[1]).start()
-
-    x_steps = [
-        functools.partial(x_stage, zz, j)
-        for hf in range(2)
-        for j in range(1, ny + 1)
-        for zz in range(hf * nz // 2, (hf + 1) * nz // 2)
-    ]
+
     fillers = [functools.partial(w_forward, i) for i in range(1, W_CHUNKS)]
     fillers += [functools.partial(weights_of, j) for j in range(1, ny)]
     fillers += [functools.partial(weights_other, j) for j in range(1, ny)]
     fillers += [functools.partial(backward, h) for h in range(heads)]
+    x_steps = [item for n in range(2) for item in x_order(n)]
+    slots = len(x_steps) - half_z
     done = 0
     for n, x_step in enumerate(x_steps):
-        x_step()
-        until = (n + 1) * len(fillers) // len(x_steps)
+        x_stage(*x_step)
+        until = (n + 1) * len(fillers) // slots
         for filler in fillers[done:until]:
             filler()
-        done = until
+        done = max(done, until)
+        passed = n + 1 - ny * half_z
+        if passed > 0 and passed % half_z == 0 and passed < ny * half_z:
+            j = passed // half_z
+            y_send[j - 1] = z_stage(j).astype(bf16)
+            send(y_send.at[j - 1], y_recv.at[y], ys_sem.at[j - 1], yr_sem.at[y], y_dev(j))
 
     factor = state["factor"]
-    for j in range(1, ny):
-        y_send[j - 1] = z_stage(j).astype(bf16)
-        send(y_send.at[j - 1], y_recv.at[y], ys_sem.at[j - 1], yr_sem.at[y], y_dev(j))
     total = z_stage(ny)
     for j in range(1, ny):
         src = y_of(j)
@@ -298,21 +315,18 @@
         remote(ref, ref, ys_sem.at[j - 1], yr_sem.at[src], y_dev(j)).wait_recv()
         total = total + ref[...].astype(f32)
     gw[...] = total * factor
-    pltpu.make_async_copy(gw, gw_hbm, out_sem.at[2]).start()
 
     for copy in sends:
         copy.wait_send()
-    for zz in range(nz):
-        for yy in range(ny):
-            @pl.when(zz != z)
-            def _(zz=zz, yy=yy):
-                remote(z_send.at[zz, yy], z_recv.at[z, yy], zs_sem.at[zz, yy], zr_sem.at[z, yy],
-                       (zz * 2 + x, fs)).wait_send()
-    for s in range(nf):
-        pltpu.make_async_copy(bo.at[s], bo_hbm.at[:, pl.ds(s * cols, cols)], bo_sem.at[s]).wait()
-    pltpu.make_async_copy(gq, gq_hbm, out_sem.at[0]).wait()
-    pltpu.make_async_copy(gkv, gkv_hbm, out_sem.at[1]).wait()
-    pltpu.make_async_copy(gw, gw_hbm, out_sem.at[2]).wait()
+
+
+def copy_out(a, b, c, d, a_hbm, b_hbm, c_hbm, d_hbm, sem):
+    pairs = [(a, a_hbm), (b, b_hbm), (c, c_hbm), (d, d_hbm)]
+    copies = [pltpu.make_async_copy(*pair, sem.at[i]) for i, pair in enumerate(pairs)]
+    for copy in copies:
+        copy.start()
+    for copy in copies:
+        copy.wait()
 
 
 def fused(nd, nf, queries, keys_values, seg_ids, in_resp, advantage, out_weight, upstream):
@@ -322,44 +336,54 @@
     cols = out_weight.shape[1]
     rows = depth // nd
     nz, ny = nd // 2, nf // 2
+    hbm_spec = pl.BlockSpec(memory_space=pltpu.HBM)
     any_spec = pl.BlockSpec(memory_space=pl.ANY)
     V, D = pltpu.VMEM, pltpu.SemaphoreType.DMA
-    return pl.pallas_call(
+    results = pl.pallas_call(
         functools.partial(fused_kernel, (nd, nf, tok, heads, head, rows, cols)),
         out_shape=(
-            jax.ShapeDtypeStruct((tok, nf * cols), bf16),
-            jax.ShapeDtypeStruct((tok, depth), bf16),
-            jax.ShapeDtypeStruct((tok, 2 * head), bf16),
-            jax.ShapeDtypeStruct((rows, cols), f32),
+            pltpu.VMEM((tok, nf * cols), bf16),
+            pltpu.VMEM((tok, depth), bf16),
+            pltpu.VMEM((tok, 2 * head), bf16),
+            pltpu.VMEM((rows, cols), f32),
         ),
-        in_specs=[any_spec] * 7,
-        out_specs=(any_spec,) * 4,
+        in_specs=[hbm_spec] * 7,
+        out_specs=(pl.BlockSpec(memory_space=pltpu.VMEM),) * 4,
         scratch_shapes=[
             V((tok, depth), bf16), V((tok, 2 * head), bf16),
             V((1, tok), jnp.int32), V((1, tok), jnp.int32), V((1, tok), jnp.int32),
             V((tok, nf * cols), bf16),
-            V((nf, depth, cols), bf16), V((nf, tok, cols), bf16), V((nf, tok, cols), bf16),
+            V((nf, depth, cols), bf16), V((nf, tok, cols), bf16),
             V((tok, depth), bf16), V((heads, tok, tok), bf16), V((tok, depth), f32),
             V((tok, tok), f32), V((6, 8, 128), f32),
-            V((tok, depth), bf16), V((tok, 2 * head), bf16), V((rows, cols), f32),
             V((nf, nd, rows, cols), bf16), V((ny, nd, rows, cols), bf16),
             V((nz, ny, rows, cols), bf16), V((nz, ny, rows, cols), bf16),
             V((nz, ny, rows, cols), bf16), V((nz, ny, rows, cols), bf16),
             V((ny, rows, cols), bf16), V((ny, rows, cols), bf16),
             V((ny, 8, 128), f32), V((nz, 8, 128), f32),
-            D((7,)), D((3,)), D((nf,)),
+            D((7,)),
             D((nf, W_CHUNKS)), D((nf, W_CHUNKS)),
             D((2, ny)), D((2, ny)), D((nz, ny)), D((nz, ny)), D((nz, ny)), D((nz, ny)),
             D((ny,)), D((ny,)),
             D((2,)), D((2,)), D((ny,)), D((ny,)), D((nz,)), D((nz,)),
         ],
         compiler_params=pltpu.CompilerParams(
-            collective_id=0, has_side_effects=True, vmem_limit_bytes=48 * 1024 * 1024
+            collective_id=0, has_side_effects=True, vmem_limit_bytes=60 * 1024 * 1024
         ),
     )(
-        queries, keys_values, seg_ids.reshape(1, -1), in_resp.reshape(1, -1),
-        advantage.reshape(1, -1), out_weight, upstream,
+        *[pltpu.with_memory_space_constraint(a, pltpu.HBM) for a in (
+            queries, keys_values, seg_ids.reshape(1, -1), in_resp.reshape(1, -1),
+            advantage.reshape(1, -1), out_weight, upstream,
+        )]
     )
+    return pl.pallas_call(
+        copy_out,
+        out_shape=tuple(pltpu.HBM(r.shape, r.dtype) for r in results),
+        in_specs=[pl.BlockSpec(memory_space=pltpu.VMEM)] * 4,
+        out_specs=(any_spec,) * 4,
+        scratch_shapes=[D((4,))],
+        compiler_params=pltpu.CompilerParams(vmem_limit_bytes=4 * 1024 * 1024),
+    )(*results)
 
 
 def attend_forward(q_rows, kv_rows, seg_rows):

time: 48.4 us -> 34.3 us (0.71)
  the two profiles are of different devices: /device:TPU:24 before, /device:TPU:0 now
where the time goes in v2:
time: 34.3 us; the launch traced here: 34.1 us
  Pallas kernels  33.5 us (98%)
  between operations  0.64 us (2%)
    pallas_call x1, Pallas kernels, fused(): pl.pallas_call(functools.partial(fused_kernel, (nd, nf, tok, heads, head,...  32.4 us
    pallas_call x1, Pallas kernels, fused(): pl.pallas_call(copy_out, out_shape=tuple((pltpu.HBM(r.shape, r.dtype) for...  1.13 us

profile of v2, /device:TPU:0, one launch (start us, length us, event | category | flops | bytes accessed | tf_op | source)
XLA Modules:
  0.0 34.1 jit_solution(3900868481919196015)
XLA Ops:
  0.6 32.4 %shard_map.102 = (bf16[256,1536]{1,0:T(8,128)(2,1)S(1)}, bf16[256,768]{1,0:T(8,128)(2,1)S(1)}, bf16[256,256]{1,0:T(8,128)(2,1)S(1)}, f32[96,384]{1,0:T(8,128)S(1)}) custom-call(bf16[256,768]{1,0:T(8,128)(2,1)} %q_hbm.1, bf16[256,256]{1,0:T(8,128)(2,1)} %kv_hbm.1, s32[1,256]{1,0:T(1,128)} %bitcast.3, s32[1,256]{1,0:T(1,128)} %bitcast.4, s32[1,256]{1,0:T(1,128)} %bitcast.5, ...), custom_call_target="tpu_custom_call" | custom-call | tf_op jit(solution)/shard_map/pallas_call | solution.py:342
  33.0 1.1 %shard_map.103 = (bf16[256,1536]{1,0:T(8,128)(2,1)}, bf16[256,768]{1,0:T(8,128)(2,1)}, bf16[256,256]{1,0:T(8,128)(2,1)}, f32[96,384]{1,0:T(8,128)}) custom-call(bf16[256,1536]{1,0:T(8,128)(2,1)S(1)} %get-tuple-element.8.a, bf16[256,768]{1,0:T(8,128)(2,1)S(1)} %get-tuple-element.9.b, bf16[256,256]{1,0:T(8,128)(2,1)S(1)} %get-tuple-element.10.c, ...), custom_call_target="tpu_custom_call" | custom-call | tf_op jit(solution)/shard_map/pallas_call | solution.py:379

commit v3 on v2

--- a/solution.py
+++ b/solution.py
@@ -288,24 +288,31 @@
             gkv[:, :head] = (state["gk"] * (scale * factor)).astype(bf16)
             gkv[:, head:] = (state["gv"] * factor).astype(bf16)
 
-    fillers = [functools.partial(w_forward, i) for i in range(1, W_CHUNKS)]
-    fillers += [functools.partial(weights_of, j) for j in range(1, ny)]
-    fillers += [functools.partial(weights_other, j) for j in range(1, ny)]
-    fillers += [functools.partial(backward, h) for h in range(heads)]
     x_steps = [item for n in range(2) for item in x_order(n)]
-    slots = len(x_steps) - half_z
-    done = 0
+    plan = [[] for _ in x_steps]
+
+    def place(eighth, work):
+        plan[eighth * len(x_steps) // 8].append(work)
+
+    place(1, lambda: w_forward(1))
+    for i in range(2, W_CHUNKS):
+        place(3, functools.partial(w_forward, i))
+    for j in range(1, ny):
+        place(4, functools.partial(weights_of, j))
+    for j in range(1, ny):
+        place(5, functools.partial(weights_other, j))
+    for h in range(heads):
+        place(6 if h < half_heads else 6, functools.partial(backward, h))
     for n, x_step in enumerate(x_steps):
         x_stage(*x_step)
-        until = (n + 1) * len(fillers) // slots
-        for filler in fillers[done:until]:
-            filler()
-        done = max(done, until)
         passed = n + 1 - ny * half_z
         if passed > 0 and passed % half_z == 0 and passed < ny * half_z:
             j = passed // half_z
             y_send[j - 1] = z_stage(j).astype(bf16)
             send(y_send.at[j - 1], y_recv.at[y], ys_sem.at[j - 1], yr_sem.at[y], y_dev(j))
+
+        for work in plan[n]:
+            work()
 
     factor = state["factor"]
     total = z_stage(ny)

time: 34.3 us -> 32.5 us (0.948)
  Pallas kernels: 33.5 us -> 31.7 us
    pallas_call x1, Pallas kernels: 32.4 us -> 30.6 us  [fused(): pl.pallas_call(functools.partial(fused_kernel, (nd, nf, tok, heads, head,...]
where the time goes in v3:
time: 32.5 us; the launch traced here: 32.4 us
  Pallas kernels  31.7 us (98%)
  between operations  0.64 us (2%)
    pallas_call x1, Pallas kernels, fused(): pl.pallas_call(functools.partial(fused_kernel, (nd, nf, tok, heads, head,...  30.6 us
    pallas_call x1, Pallas kernels, fused(): pl.pallas_call(copy_out, out_shape=tuple((pltpu.HBM(r.shape, r.dtype) for...  1.13 us

profile of v3, /device:TPU:0, one launch (start us, length us, event | category | flops | bytes accessed | tf_op | source)
XLA Modules:
  0.0 32.4 jit_solution(68764369683768890)
XLA Ops:
  0.6 30.6 %shard_map.102 = (bf16[256,1536]{1,0:T(8,128)(2,1)S(1)}, bf16[256,768]{1,0:T(8,128)(2,1)S(1)}, bf16[256,256]{1,0:T(8,128)(2,1)S(1)}, f32[96,384]{1,0:T(8,128)S(1)}) custom-call(bf16[256,768]{1,0:T(8,128)(2,1)} %q_hbm.1, bf16[256,256]{1,0:T(8,128)(2,1)} %kv_hbm.1, s32[1,256]{1,0:T(1,128)} %bitcast.3, s32[1,256]{1,0:T(1,128)} %bitcast.4, s32[1,256]{1,0:T(1,128)} %bitcast.5, ...), custom_call_target="tpu_custom_call" | custom-call | tf_op jit(solution)/shard_map/pallas_call | solution.py:349
  31.2 1.1 %shard_map.103 = (bf16[256,1536]{1,0:T(8,128)(2,1)}, bf16[256,768]{1,0:T(8,128)(2,1)}, bf16[256,256]{1,0:T(8,128)(2,1)}, f32[96,384]{1,0:T(8,128)}) custom-call(bf16[256,1536]{1,0:T(8,128)(2,1)S(1)} %get-tuple-element.8.a, bf16[256,768]{1,0:T(8,128)(2,1)S(1)} %get-tuple-element.9.b, bf16[256,256]{1,0:T(8,128)(2,1)S(1)} %get-tuple-element.10.c, ...), custom_call_target="tpu_custom_call" | custom-call | tf_op jit(solution)/shard_map/pallas_call | solution.py:386
